TPU v7x, 32 devices: a whole 2x2x4 slice. The times are simulated.
32 devices in a mesh: chan: 4 (over y, x), tm: 8 (over z, core).
Axes of the slice: x: 2, y: 2, z: 4, core: 2. Of those that a mesh axis runs over, the one named last changes fastest.
Arguments:
- volts: bfloat16 [4, 2048, 512], P('chan', 'tm'), may hold values from -120 to 120
- picks: int32 [4, 8], P('chan'), may hold values from 0 to 63, as said below
- angles: float32 [64], replicated, may hold values from -3.140625 to 3.140625
Outputs:
- cleaned: float32 [4, 2048, 512], P('chan', 'tm')
Inputs may be any that keep to these rules, and one draw needn't show every extreme that they name: No index appears twice among all groups' picks.
All inputs are finite; a program needn't handle non-finite values.
Results may differ from a plain program's by a relative error of at most 0.00035.
Values sent between devices are 32-bit elements; how exact they have to be, the bound alone decides.
No kernel may reach another device: no remote copies, remote signals or barrier semaphores. Data moves between devices by JAX's collectives and lax.ppermute only.
A program may use at most 64 MiB of HBM per device.

v0:
```python
import jax
import jax.numpy as jnp
from jax import lax
from jax.sharding import PartitionSpec as P

SEG = 256
HORIZON = 256
WSTEPS = 4


LOADING = 0.1
STEER_LOADING = 0.05
TINY_LEVEL = 1e-06
PRECISE = lax.Precision.HIGHEST


def steering_rows(angle_sel, antennas):
    position = jnp.arange(antennas).astype(jnp.float32)
    phase = jnp.pi * jnp.sin(angle_sel)[:, None] * position[None, :]
    norming = jnp.sqrt(jnp.asarray(antennas, jnp.float32))
    real_part = jnp.cos(phase) / norming
    imag_part = jnp.sin(phase) / norming
    upper = jnp.concatenate([real_part, imag_part], axis=1)
    lower = jnp.concatenate([-imag_part, real_part], axis=1)
    return jnp.concatenate([upper, lower], axis=0)


def null_factor(steer_rows):
    count = steer_rows.shape[0]
    steer_gram = jnp.dot(steer_rows, steer_rows.T, precision=PRECISE) + STEER_LOADING * jnp.eye(
        count, dtype=jnp.float32
    )
    chol_gram = jnp.linalg.cholesky(steer_gram)
    return jax.scipy.linalg.solve_triangular(chol_gram, steer_rows, lower=True)


def halves(full_gram, antennas):
    real_half = full_gram[:antennas, :antennas] + full_gram[antennas:, antennas:]
    imag_half = full_gram[antennas:, :antennas] - full_gram[:antennas, antennas:]
    return jnp.stack([real_half, imag_half])


def whiten(covariance, band_level, projected):
    antennas = covariance.shape[1]
    upper = jnp.concatenate([covariance[0], -covariance[1]], axis=1)
    lower = jnp.concatenate([covariance[1], covariance[0]], axis=1)
    loaded = jnp.concatenate([upper, lower], axis=0) / band_level + LOADING * jnp.eye(
        2 * antennas, dtype=jnp.float32
    )
    omega = 1.0 / jnp.sqrt(jnp.sum(loaded * loaded))
    iterate = omega * projected
    for sweep in range(WSTEPS):
        iterate = iterate + omega * (projected - jnp.dot(iterate, loaded, precision=PRECISE))
    return iterate


def on_device(volts, picks, angles):
    voltage = volts[0]
    antennas = voltage.shape[1] // 2
    segments = voltage.shape[0] // SEG
    forget = jnp.asarray(1.0 - 1.0 / HORIZON, jnp.float32)
    forget_dev = jnp.power(forget, jnp.asarray(segments, jnp.float32))
    pieces = voltage.reshape(segments, SEG, 2 * antennas)
    seg_grams = jnp.einsum("sli,slj->sij", pieces, pieces, preferred_element_type=jnp.float32)
    powers = (segments - 1 - jnp.arange(segments)).astype(jnp.float32)
    own_term = jnp.einsum("s,sij->ij", jnp.power(forget, powers), seg_grams, precision=PRECISE)
    own_halves = halves(own_term, antennas)
    members = lax.axis_size("tm")
    sliced = own_halves.reshape(members, -1)
    received = lax.all_to_all(sliced, "tm", split_axis=0, concat_axis=0, tiled=True)
    position = jnp.arange(members)
    distance = position[:, None] - position[None, :]
    weights = jnp.where(
        distance >= 0,
        jnp.power(forget_dev, jnp.maximum(distance, 0).astype(jnp.float32)),
        jnp.zeros((), jnp.float32),
    )
    prefix = jnp.dot(weights, received, precision=PRECISE)
    returned = lax.all_to_all(prefix, "tm", split_axis=0, concat_axis=0, tiled=True)
    covariance = returned.reshape(own_halves.shape)
    power_level = jnp.trace(covariance[0]) / antennas
    band_level = lax.psum(power_level, "chan") / lax.axis_size("chan") + TINY_LEVEL
    selector = (picks[0][:, None] == jnp.arange(angles.shape[0], dtype=jnp.int32)[None, :]).astype(
        jnp.float32
    )
    angle_sel = jnp.dot(selector, angles, precision=PRECISE)
    null_rows = null_factor(steering_rows(angle_sel, antennas))
    volt_float = voltage.astype(jnp.float32)
    inner = jnp.dot(volt_float, null_rows.T, precision=PRECISE)
    projected = volt_float - jnp.dot(inner, null_rows, precision=PRECISE)
    cleaned = whiten(covariance, band_level, projected)
    return cleaned[None]


def solution(mesh):
    placed = (P("chan", "tm", None), P("chan", None), P())
    return jax.shard_map(
        on_device, mesh=mesh, in_specs=placed, out_specs=P("chan", "tm", None), check_vma=False
    )
```

profile of v0, /device:TPU:0, one launch (start us, length us, event | category | flops | bytes accessed | tf_op | source)
XLA Modules:
  0.0 66.9 jit_solution(119287535334959372)
XLA Ops:
  0.0 0.0 copy-start
  0.0 1.4 %fusion.20 = f32[512,512]{1,0:T(8,128)S(1)} fusion(bf16[1,256,512]{2,1,0:T(8,128)(2,1)} %param.3), kind=kOutput, calls=%fused_computation.35 | convolution fusion | flops 134217728 | bytes 1310720 | tf_op jit(solution)/shard_map/sli,slj->sij/dot_general | solution.py:64
  1.4 0.1 fusion.16
  1.5 1.3 %all_to_all.19 = f32[8,1,16384]{2,1,0:T(1,128)} reshape(f32[2,256,256]{2,1,0:T(8,128)S(1)} %pad_maximum_fusion) | data formatting | bytes 1048576 | tf_op jit(solution)/shard_map/all_to_all | solution.py:70
  2.8 6.4 %all-to-all-start = ((f32[8,1,16384]{2,1,0:T(1,128)}), f32[8,1,16384]{2,1,0:T(1,128)S(1)}, u32[]{:S(2)}, u32[]{:S(2)}) async-start(f32[8,1,16384]{2,1,0:T(1,128)} %all_to_all.19), calls=%async_computation | async-start | bytes 1048576 | tf_op jit(solution)/shard_map/all_to_all | solution.py:70
  9.2 0.0 copy-start.2
  9.2 0.0 copy-done
  9.2 0.6 copy-done.2
  9.8 0.2 fusion.10
  10.1 0.1 fusion.27
  10.2 0.1 fusion.24
  10.3 0.1 copy.7
  10.4 1.5 %cholesky.16 = f32[16,16]{1,0:T(8,128)S(1)} custom-call(f32[16,16]{1,0:T(8,128)S(1)} %fusion.30), custom_call_target="Cholesky" | custom-call | tf_op jit(solution)/shard_map/jit(cholesky)/cholesky | solution.py:33
  11.9 0.7 %compare_reduce_fusion = pred[]{:T(512)} fusion(f32[16]{0:T(128)S(1)} %select_reduce_fusion), kind=kLoop, calls=%fused_computation.69 | loop fusion | flops 31 | bytes 65 | tf_op jit(solution)/shard_map/jit(cholesky)/cholesky | solution.py:33
  12.7 0.1 broadcast_bitcast_fusion
  12.8 11.7 %all-to-all-done = f32[8,1,16384]{2,1,0:T(1,128)S(1)} async-done(((f32[8,1,16384]{2,1,0:T(1,128)}), f32[8,1,16384]{2,1,0:T(1,128)S(1)}, u32[]{:S(2)}, u32[]{:S(2)}) %all-to-all-start) | async-done | bytes 524320 | tf_op jit(solution)/shard_map/all_to_all | solution.py:70
  24.5 0.8 %convolution_bitcast_fusion = f32[8,1,16384]{2,0,1:T(8,128)S(1)} fusion(f32[8,1,16384]{2,1,0:T(1,128)S(1)} %all-to-all-done), kind=kOutput, calls=%fused_computation | convolution fusion | flops 12583232 | bytes 1048576 | tf_op jit(solution)/shard_map/dot_general | solution.py:78
  25.3 1.3 %copy.6 = f32[8,1,16384]{2,1,0:T(1,128)} copy(f32[8,1,16384]{2,0,1:T(8,128)S(1)} %convolution_bitcast_fusion) | data formatting | bytes 1048576 | tf_op jit(solution)/shard_map/all_to_all | solution.py:79
  26.6 3.5 %all-to-all-start.1 = ((f32[8,1,16384]{2,1,0:T(1,128)}), f32[8,1,16384]{2,1,0:T(1,128)S(1)}, u32[]{:S(2)}, u32[]{:S(2)}) async-start(f32[8,1,16384]{2,1,0:T(1,128)} %copy.6), calls=%async_computation.1 | async-start | bytes 1048576 | tf_op jit(solution)/shard_map/all_to_all | solution.py:79
  30.1 0.7 %fusion.25 = f32[1,16,16]{2,1,0:T(8,128)S(1)} fusion(f32[16,16]{1,0:T(8,128)S(1)} %cholesky.16, pred[]{:T(512)} %compare_reduce_fusion), kind=kLoop, calls=%fused_computation.46 | loop fusion | flops 1024 | bytes 2049 | tf_op jit(solution)/shard_map/jit(_solve_triangular)/triangular_solve | solution.py:34
  30.8 1.2 %custom-call.7 = f32[1,16,16]{1,2,0:T(8,128)S(1)} custom-call(f32[1,16,16]{2,1,0:T(8,128)S(1)} %fusion.25), custom_call_target="InvertDiagBlocksLowerTriangular" | custom-call | tf_op jit(solution)/shard_map/jit(_solve_triangular)/triangular_solve | solution.py:34
  32.1 0.0 copy-start.1
  32.1 0.2 copy.10
  32.3 0.2 fusion.23
  32.5 0.5 copy-done.1
  33.0 0.3 fusion.18
  33.3 0.7 convolution_subtract_fusion.4
  34.0 11.4 %all-to-all-done.1 = f32[8,1,16384]{2,1,0:T(1,128)S(1)} async-done(((f32[8,1,16384]{2,1,0:T(1,128)}), f32[8,1,16384]{2,1,0:T(1,128)S(1)}, u32[]{:S(2)}, u32[]{:S(2)}) %all-to-all-start.1) | async-done | bytes 524320 | tf_op jit(solution)/shard_map/all_to_all | solution.py:79
  45.4 1.5 %slice_reduce_fusion = (f32[4,16384]{1,0:T(4,128)S(1)}, f32[4,16384]{1,0:T(4,128)S(1)}, f32[4,1,16384]{2,1,0:T(1,128)S(1)}) fusion(f32[8,1,16384]{2,1,0:T(1,128)S(1)} %all-to-all-done.1), kind=kLoop, calls=%fused_computation.26 | loop fusion | bytes 1310720 | tf_op jit(solution)/shard_map/slice | solution.py:45
  46.9 0.2 squeeze.5
  47.1 0.8 %fusion.17 = f32[]{:T(128)} fusion(f32[4,1,16384]{2,1,0:T(1,128)S(1)} %get-tuple-element.9, s32[4,16384]{1,0:T(4,128)S(1)} %bitcast.54, s32[16384]{0:T(1024)S(1)} %bitcast.55), kind=kLoop, calls=%fused_computation.32 | loop fusion | flops 196607 | bytes 589828 | tf_op jit(solution)/shard_map/jit(trace)/reduce_sum | solution.py:81
  48.6 10.4 %psum.7 = f32[]{:T(128)} all-reduce(f32[]{:T(128)S(6)} %div.27), channel_id=1, replica_groups=mesh['chan'=4,'tm'=8] {'chan'}, use_global_device_ids=true, to_apply=%region_1.2 | all-reduce | flops 1 | bytes 8 | tf_op jit(solution)/shard_map/psum | solution.py:82
  59.0 0.2 squeeze.4
  59.9 0.9 %multiply_reduce_fusion = f32[]{:T(128)} fusion(f32[]{:T(128)S(6)} %add.43, f32[256,256]{1,0:T(8,128)S(1)} %squeeze.4, f32[256,256]{1,0:T(8,128)S(1)} %squeeze.5, f32[256,256]{1,0:T(8,128)S(1)} %neg.6), kind=kLoop, calls=%fused_computation.20 | loop fusion | flops 2359295 | bytes 786440 | tf_op jit(solution)/shard_map/reduce_sum | solution.py:50
  61.4 1.2 %fusion.1 = f32[256,512]{1,0:T(8,128)S(1)} fusion(f32[256,512]{1,0:T(8,128)S(1)} %convolution_subtract_fusion.4, f32[]{:T(128)S(6)} %sqrt.3, f32[256,256]{1,0:T(8,128)S(1)} %squeeze.4, f32[256,256]{1,0:T(8,128)S(1)} %squeeze.5, f32[256,256]{1,0:T(8,128)S(1)} %neg.6, f32[]{:T(128)S(6)} %add.43), kind=kOutput, calls=%fused_computation.6 | convolution fusion | flops 807796736 | bytes 1835016 | tf_op jit(solution)/shard_map/dot_general | solution.py:53
  62.6 1.1 %fusion.3 = f32[256,512]{1,0:T(8,128)S(1)} fusion(f32[256,512]{1,0:T(8,128)S(1)} %fusion.1, f32[256,512]{1,0:T(8,128)S(1)} %convolution_subtract_fusion.4, f32[]{:T(128)S(6)} %sqrt.3, f32[256,256]{1,0:T(8,128)S(1)} %squeeze.4, f32[256,256]{1,0:T(8,128)S(1)} %squeeze.5, f32[256,256]{1,0:T(8,128)S(1)} %neg.6, f32[]{:T(128)S(6)} %add.43), kind=kOutput, calls=%fused_computation.8 | convolution fusion | flops 807534592 | bytes 2359304 | tf_op jit(solution)/shard_map/dot_general | solution.py:53
  63.8 1.1 %fusion.5 = f32[256,512]{1,0:T(8,128)S(1)} fusion(f32[256,512]{1,0:T(8,128)S(1)} %fusion.3, f32[256,512]{1,0:T(8,128)S(1)} %convolution_subtract_fusion.4, f32[]{:T(128)S(6)} %sqrt.3, f32[256,256]{1,0:T(8,128)S(1)} %squeeze.4, f32[256,256]{1,0:T(8,128)S(1)} %squeeze.5, f32[256,256]{1,0:T(8,128)S(1)} %neg.6, f32[]{:T(128)S(6)} %add.43), kind=kOutput, calls=%fused_computation.10 | convolution fusion | flops 807534592 | bytes 2359304 | tf_op jit(solution)/shard_map/dot_general | solution.py:53
  64.9 1.9 %fusion.8 = f32[1,256,512]{2,1,0:T(8,128)} fusion(f32[256,512]{1,0:T(8,128)S(1)} %fusion.5, f32[256,512]{1,0:T(8,128)S(1)} %convolution_subtract_fusion.4, f32[]{:T(128)S(6)} %sqrt.3, f32[256,256]{1,0:T(8,128)S(1)} %squeeze.4, f32[256,256]{1,0:T(8,128)S(1)} %squeeze.5, f32[256,256]{1,0:T(8,128)S(1)} %neg.6, f32[]{:T(128)S(6)} %add.43), kind=kOutput, calls=%fused_computation.13 | convolution fusion | flops 807534592 | bytes 2359304 | tf_op jit(solution)/shard_map/dot_general | solution.py:53
  (8 shorter events, 0.1 us)
Async XLA Ops:
  0.0 9.2 %copy-start = (f32[64]{0:T(128)S(1)}, f32[64]{0:T(128)}, u32[]{:S(2)}) copy-start(f32[64]{0:T(128)} %param.5) | copy-start | bytes 772
  2.8 21.7 %all-to-all-start = ((f32[8,1,16384]{2,1,0:T(1,128)}), f32[8,1,16384]{2,1,0:T(1,128)S(1)}, u32[]{:S(2)}, u32[]{:S(2)}) async-start(f32[8,1,16384]{2,1,0:T(1,128)} %all_to_all.19), calls=%async_computation | async-start | bytes 1048576 | tf_op jit(solution)/shard_map/all_to_all | solution.py:70
  9.2 0.7 copy-start.2
  26.6 18.8 %all-to-all-start.1 = ((f32[8,1,16384]{2,1,0:T(1,128)}), f32[8,1,16384]{2,1,0:T(1,128)S(1)}, u32[]{:S(2)}, u32[]{:S(2)}) async-start(f32[8,1,16384]{2,1,0:T(1,128)} %copy.6), calls=%async_computation.1 | async-start | bytes 1048576 | tf_op jit(solution)/shard_map/all_to_all | solution.py:79
  32.1 1.0 %copy-start.1 = (bf16[1,256,512]{2,1,0:T(8,128)(2,1)S(1)}, bf16[1,256,512]{2,1,0:T(8,128)(2,1)}, u32[]{:S(2)}) copy-start(bf16[1,256,512]{2,1,0:T(8,128)(2,1)} %param.3) | copy-start | bytes 786436
where the time goes:
time: 67.3 us; the launch traced here: 66.9 us
  waiting for transfers between devices  23.1 us (34%)
  blocking collectives  10.4 us (15%)
  starting transfers between devices  9.85 us (15%)
  matrix products  9.1 us (14%)
  local copies, waits for them, and re-layouts  6.11 us (9%)
  other arithmetic  6.09 us (9%)
  between operations  2.17 us (3%)
    all_to_all x1, waiting for transfers between devices, on_device(): lax.all_to_all(sliced, 'tm', split_axis=0, concat_axis=0, tiled=True)  11.7 us
    all_to_all x1, waiting for transfers between devices, on_device(): lax.all_to_all(prefix, 'tm', split_axis=0, concat_axis=0, tiled=True)  11.4 us
    psum x1, blocking collectives, on_device(): lax.psum(power_level, 'chan') / lax.axis_size('chan') + TINY_LEVEL  10.4 us
    all_to_all x1, starting transfers between devices, on_device(): lax.all_to_all(sliced, 'tm', split_axis=0, concat_axis=0, tiled=True)  6.35 us
    dot_general x4, matrix products, whiten(): jnp.dot(iterate, loaded, precision=PRECISE)  5.41 us
    all_to_all x1, starting transfers between devices, on_device(): lax.all_to_all(prefix, 'tm', split_axis=0, concat_axis=0, tiled=True)  3.49 us
    another operation x3, other arithmetic, null_factor(): chol_gram = jnp.linalg.cholesky(steer_gram)  2.22 us
    another operation x2, other arithmetic, null_factor(): return jax.scipy.linalg.solve_triangular(chol_gram, steer_rows, lower=True)  1.92 us
  transfers between devices with their start and end apart: 2, of which 2 were waited for; matrix products, arithmetic and copies ran while one was open for 9% of the time, Pallas kernels for 0%

commit v1 on v0

v1 whole, which is shorter than its diff:
```python
import jax
import jax.numpy as jnp
from jax import lax
from jax.experimental import pallas as pl
from jax.experimental.pallas import tpu as pltpu
from jax.sharding import PartitionSpec as P

SEG = 256
HORIZON = 256
LOADING = 0.1
STEER_LOADING = 0.05
TINY_LEVEL = 1e-06
PRECISE = lax.Precision.HIGHEST
RADIX = 4
F32 = jnp.float32
BF16 = jnp.bfloat16
VM = pl.BlockSpec(memory_space=pltpu.VMEM)
SM = pl.BlockSpec(memory_space=pltpu.SMEM)


def gram_kernel(parity_ref, volts_ref, keep_ref, give_ref, power_ref, mixed_ref):
    antennas = volts_ref.shape[1] // 2
    segments = volts_ref.shape[0] // SEG
    half = antennas // 2
    forget = 1.0 - 1.0 / HORIZON
    mixed = None
    for seg in range(segments):
        a = volts_ref[seg * SEG : (seg + 1) * SEG, :antennas]
        b = volts_ref[seg * SEG : (seg + 1) * SEG, antennas:]
        left = jnp.concatenate([a, b, b, -a], axis=0)
        right = jnp.concatenate([a, b, a, b], axis=0)
        term = lax.dot_general(
            left, right, (((0,), (0,)), ((), ())), preferred_element_type=F32
        )
        mixed = term if mixed is None else forget * mixed + term
    mixed_ref[...] = mixed
    row = lax.broadcasted_iota(jnp.int32, mixed.shape, 0)
    column = lax.broadcasted_iota(jnp.int32, mixed.shape, 1)
    trace = jnp.sum(jnp.where(row == column, mixed, 0.0))
    power_ref[...] = jnp.full(power_ref.shape, trace / antennas, F32)
    parity = parity_ref[0]
    keep_ref[...] = mixed_ref[pl.ds(pl.multiple_of(parity * half, half), half), :]
    give_ref[...] = mixed_ref[pl.ds(pl.multiple_of((1 - parity) * half, half), half), :]


def split(value):
    high = value.astype(BF16)
    return high, (value - high.astype(F32)).astype(BF16)


def dot3(left, right):
    (lh, ll), (rh, rl) = left, right
    return (
        jnp.dot(lh, rh, preferred_element_type=F32)
        + jnp.dot(lh, rl, preferred_element_type=F32)
        + jnp.dot(ll, rh, preferred_element_type=F32)
    )


def stacked(high_low, first, second):
    return tuple(
        jnp.concatenate(
            [
                jnp.concatenate([part[first], part[second]], axis=1),
                jnp.concatenate([part[second], -part[first]], axis=1),
            ],
            axis=0,
        )
        for part in high_low
    )


def whiten_kernel(parity_ref, band_ref, own_ref, other_ref, w_ref, out_ref, mixed_ref):
    half, antennas = own_ref.shape
    parity = parity_ref[0]
    mixed_ref[pl.ds(pl.multiple_of(parity * half, half), half), :] = own_ref[...]
    mixed_ref[pl.ds(pl.multiple_of((1 - parity) * half, half), half), :] = other_ref[...]
    mixed = mixed_ref[...]
    flipped = mixed.T
    scale = 0.5 / band_ref[0:1, 0:1]
    row = lax.broadcasted_iota(jnp.int32, mixed.shape, 0)
    column = lax.broadcasted_iota(jnp.int32, mixed.shape, 1)
    re = (mixed + flipped) * scale + jnp.where(row == column, LOADING, 0.0)
    im = (mixed - flipped) * scale
    omega = 1.0 / jnp.sqrt(2.0 * jnp.sum(re * re + im * im, keepdims=True))
    a_re, a_im = omega * re, omega * im
    (rh, rl), (ih, il) = split(a_re), split(a_im)
    lhs = tuple(
        jnp.concatenate(
            [jnp.concatenate([r, -i], axis=1), jnp.concatenate([i, r], axis=1)], axis=0
        )
        for r, i in ((rh, ih), (rl, il))
    )
    a_col = jnp.concatenate([a_re, a_im], axis=0)
    a_high, a_low = jnp.concatenate([rh, ih], axis=0), jnp.concatenate([rl, il], axis=0)
    square = dot3(lhs, (a_high, a_low))
    first, second = split(square - 2.0 * a_col), split(3.0 * a_col - square)
    samples = w_ref.shape[0]
    left, right = slice(0, antennas), slice(antennas, 2 * antennas)

    def turn(u, v):
        parts = zip(split(u), split(v), strict=True)
        return tuple(
            jnp.concatenate(
                [jnp.concatenate([p, q], axis=1), jnp.concatenate([q, -p], axis=1)], axis=0
            )
            for p, q in parts
        )

    w_u, w_v = w_ref[:, left], w_ref[:, right]
    step = dot3(turn(w_u, w_v), first)
    u, v = 2.0 * w_u + step[:samples], 2.0 * w_v + step[samples:]
    step = dot3(turn(u, v), second)
    out_ref[:, left] = omega * (w_u + 2.0 * u - step[:samples])
    out_ref[:, right] = omega * (w_v + 2.0 * v - step[samples:])


def steering_rows(angle_sel, antennas):
    position = jnp.arange(antennas).astype(F32)
    phase = jnp.pi * jnp.sin(angle_sel)[:, None] * position[None, :]
    norming = jnp.sqrt(jnp.asarray(antennas, F32))
    real_part = jnp.cos(phase) / norming
    imag_part = jnp.sin(phase) / norming
    upper = jnp.concatenate([real_part, imag_part], axis=1)
    lower = jnp.concatenate([-imag_part, real_part], axis=1)
    return jnp.concatenate([upper, lower], axis=0)


def null_factor(steer_rows):
    count = steer_rows.shape[0]
    steer_gram = jnp.dot(steer_rows, steer_rows.T, precision=PRECISE) + STEER_LOADING * jnp.eye(
        count, dtype=F32
    )
    chol_gram = jnp.linalg.cholesky(steer_gram)
    return jax.scipy.linalg.solve_triangular(chol_gram, steer_rows, lower=True)


def swap_cores(value, members):
    return lax.ppermute(value, "tm", [(i, i ^ 1) for i in range(members)])


def earlier_chips(value, members, decay):
    chips = members // 2
    stride, window, total = 1, value, None
    while stride < chips:
        gained = None
        for step in range(1, RADIX):
            shift = 2 * stride * step
            if shift >= members:
                break
            got = lax.ppermute(window, "tm", [(i, i + shift) for i in range(members - shift)])
            got = got if step == 1 else decay ** (stride * (step - 1)) * got
            gained = got if gained is None else gained + got
        total = gained if total is None else total + decay ** (stride - 1) * gained
        window = window + decay**stride * gained
        stride *= RADIX
    return jnp.zeros_like(value) if total is None else total


def sum_groups(value):
    groups = lax.axis_size("chan")
    if groups & (groups - 1):
        return lax.psum(value, "chan")
    step = 1
    while step < groups:
        value = value + lax.ppermute(value, "chan", [(i, i ^ step) for i in range(groups)])
        step *= 2
    return value


def on_device(volts, picks, angles):
    voltage = volts[0]
    rows, width = voltage.shape
    antennas = width // 2
    half = antennas // 2
    segments = rows // SEG
    members = lax.axis_size("tm")
    odd = lax.axis_index("tm") % 2
    parity = odd.reshape(1).astype(jnp.int32)
    is_odd = odd == 1
    decay = (1.0 - 1.0 / HORIZON) ** segments

    keep, give, power = pl.pallas_call(
        gram_kernel,
        out_shape=(
            jax.ShapeDtypeStruct((half, antennas), F32),
            jax.ShapeDtypeStruct((half, antennas), F32),
            jax.ShapeDtypeStruct((8, 128), F32),
        ),
        in_specs=[SM, VM],
        out_specs=(VM, VM, VM),
        scratch_shapes=[pltpu.VMEM((antennas, antennas), F32)],
        cost_estimate=pl.CostEstimate(
            flops=4 * rows * width * antennas, bytes_accessed=rows * width * 2, transcendentals=0
        ),
        name="segment_gram",
    )(parity, voltage)

    got = swap_cores(give, members)
    mine, theirs = jnp.where(is_odd, 1.0, decay), jnp.where(is_odd, decay, 1.0)
    pair = mine * keep + theirs * got
    before = earlier_chips(pair, members, decay * decay)
    even_cov = decay * before + jnp.where(is_odd, got, keep)
    odd_cov = decay * decay * before + pair
    own = jnp.where(is_odd, odd_cov, even_cov)
    other = swap_cores(jnp.where(is_odd, even_cov, odd_cov), members)

    level = sum_groups(power)
    level_before = earlier_chips(level, members, decay * decay)
    got_level = swap_cores(jnp.stack([level, level_before]), members)
    level_even = jnp.where(is_odd, got_level, jnp.stack([level, level_before]))
    level_odd = jnp.where(is_odd, jnp.stack([level, level_before]), got_level)
    level_chips = decay * level_even[1] + level_odd[1]
    level_own = decay * level_chips + level_even[0]
    level_own = jnp.where(is_odd, decay * level_own + level_odd[0], level_own)
    band = level_own / lax.axis_size("chan") + TINY_LEVEL

    selector = (picks[0][:, None] == jnp.arange(angles.shape[0], dtype=jnp.int32)[None, :]).astype(F32)
    angle_sel = jnp.dot(selector, angles, precision=PRECISE)
    null_rows = null_factor(steering_rows(angle_sel, antennas))
    volt_float = voltage.astype(F32)
    inner = jnp.dot(volt_float, null_rows.T, precision=PRECISE)
    projected = volt_float - jnp.dot(inner, null_rows, precision=PRECISE)

    cleaned = pl.pallas_call(
        whiten_kernel,
        out_shape=jax.ShapeDtypeStruct((rows, width), F32),
        in_specs=[SM, VM, VM, VM, VM],
        out_specs=VM,
        scratch_shapes=[pltpu.VMEM((antennas, antennas), F32)],
        cost_estimate=pl.CostEstimate(
            flops=18 * rows * width * width, bytes_accessed=rows * width * 8, transcendentals=0
        ),
        name="whiten",
    )(parity, band, own, other, projected)
    return cleaned[None]


def solution(mesh):
    placed = (P("chan", "tm", None), P("chan", None), P())
    return jax.shard_map(
        on_device, mesh=mesh, in_specs=placed, out_specs=P("chan", "tm", None), check_vma=False
    )
```

time: 67.3 us -> 46.7 us (0.69)
  the two profiles are of different devices: /device:TPU:0 before, /device:TPU:21 now
where the time goes in v1:
time: 46.7 us; the launch traced here: 46.4 us
  waiting for transfers between devices  15.6 us (33%)
  starting transfers between devices  15.1 us (32%)
  Pallas kernels  6.63 us (14%)
  other arithmetic  5.49 us (12%)
  matrix products  2.3 us (5%)
  local copies, waits for them, and re-layouts  1.19 us (3%)
    ppermute x6, waiting for transfers between devices, earlier_chips(): lax.ppermute(window, 'tm', [(i, i + shift) for i in range(members - shift)])  13.2 us
    ppermute x6, starting transfers between devices, earlier_chips(): lax.ppermute(window, 'tm', [(i, i + shift) for i in range(members - shift)])  9.93 us
    pallas_call x1, Pallas kernels, on_device(): pl.pallas_call(whiten_kernel, out_shape=jax.ShapeDtypeStruct((rows, width...  4.6 us
    ppermute x3, starting transfers between devices, swap_cores(): return lax.ppermute(value, 'tm', [(i, i ^ 1) for i in range(members)])  3.71 us
    another operation x3, other arithmetic, null_factor(): chol_gram = jnp.linalg.cholesky(steer_gram)  2.18 us
    pallas_call x1, Pallas kernels, on_device(): pl.pallas_call(gram_kernel, out_shape=(jax.ShapeDtypeStruct((half, antenn...  2.03 us
    ppermute x2, waiting for transfers between devices, sum_groups(): lax.ppermute(value, 'chan', [(i, i ^ step) for i in range(groups)])  1.95 us
    another operation x2, other arithmetic, null_factor(): return jax.scipy.linalg.solve_triangular(chol_gram, steer_rows, lower=True)  1.83 us
  transfers between devices with their start and end apart: 11, of which 6 were waited for; matrix products, arithmetic and copies ran while one was open for 15% of the time, Pallas kernels for 0%

profile of v1, /device:TPU:21, one launch (start us, length us, event | category | flops | bytes accessed | tf_op | source)
XLA Modules:
  0.0 46.4 jit_solution(15906720029507749686)
XLA Ops:
  0.0 0.0 copy-start
  0.0 0.0 copy-start.5
  0.0 2.0 %segment_gram.1 = (f32[128,256]{1,0:T(8,128)}, f32[128,256]{1,0:T(8,128)}, f32[8,128]{1,0:T(8,128)}) custom-call(s32[1]{0:T(128)} %bitcast.parity_ref, bf16[256,512]{1,0:T(8,128)(2,1)} %bitcast.47), custom_call_target="tpu_custom_call" | custom-call | flops 134217728 | bytes 262144 | tf_op jit(solution)/shard_map/segment_gram/pallas_call | solution.py:183
  2.0 0.0 copy-start.1
  2.0 1.2 %collective-permute-start = (f32[8,128]{1,0:T(8,128)}, f32[8,128]{1,0:T(8,128)S(1)}, u32[]{:S(2)}, u32[]{:S(2)}) collective-permute-start(f32[8,128]{1,0:T(8,128)} %get-tuple-element.8), channel_id=1, source_target_pairs={{0,8},{8,0},{16,24},{24,16},{1,9},{9,1},{17,25},{25,17},{2,10},{10... | collective-permute-start | bytes 12296 | tf_op jit(solution)/shard_map/ppermute | solution.py:166
  3.3 1.0 %collective-permute-start.6 = (f32[128,256]{1,0:T(8,128)}, f32[128,256]{1,0:T(8,128)S(1)}, u32[]{:S(2)}, u32[]{:S(2)}) collective-permute-start(f32[128,256]{1,0:T(8,128)} %get-tuple-element.10), channel_id=1, source_target_pairs={{0,1},{1,0},{2,3},{3,2},{4,5},{5,4},{6,7},{7,6},{8,9},{9,8},{10,11... | collective-permute-start | bytes 393224 | tf_op jit(solution)/shard_map/ppermute | solution.py:139
  4.2 0.0 copy-done
  4.2 0.0 copy-done.5
  4.2 0.2 fusion.1
  4.5 0.1 fusion.6
  4.6 0.1 fusion.3
  4.7 0.1 copy.4
  4.8 1.5 %cholesky.16 = f32[16,16]{1,0:T(8,128)S(1)} custom-call(f32[16,16]{1,0:T(8,128)S(1)} %fusion.9), custom_call_target="Cholesky" | custom-call | tf_op jit(solution)/shard_map/jit(cholesky)/cholesky | solution.py:134
  6.3 0.7 %compare_reduce_fusion = pred[]{:T(512)} fusion(f32[16]{0:T(128)S(1)} %select_reduce_fusion), kind=kLoop, calls=%fused_computation.43 | loop fusion | flops 31 | bytes 65 | tf_op jit(solution)/shard_map/jit(cholesky)/cholesky | solution.py:134
  7.0 0.6 %fusion.4 = f32[1,16,16]{2,1,0:T(8,128)S(1)} fusion(f32[16,16]{1,0:T(8,128)S(1)} %cholesky.16, pred[]{:T(512)} %compare_reduce_fusion), kind=kLoop, calls=%fused_computation.16 | loop fusion | flops 1024 | bytes 2049 | tf_op jit(solution)/shard_map/jit(_solve_triangular)/triangular_solve | solution.py:135
  7.6 1.2 %custom-call.7 = f32[1,16,16]{1,2,0:T(8,128)S(1)} custom-call(f32[1,16,16]{2,1,0:T(8,128)S(1)} %fusion.4), custom_call_target="InvertDiagBlocksLowerTriangular" | custom-call | tf_op jit(solution)/shard_map/jit(_solve_triangular)/triangular_solve | solution.py:135
  8.8 0.0 copy-start.3
  8.8 0.2 fusion.2
  9.1 0.0 collective-permute-done
  9.1 0.4 copy-done.3
  9.5 0.2 collective-permute-start.1
  9.8 0.0 copy-done.1
  9.8 0.3 fusion.21
  10.1 1.9 %collective-permute-done.1 = f32[8,128]{1,0:T(8,128)S(1)} collective-permute-done((f32[8,128]{1,0:T(8,128)S(1)}, f32[8,128]{1,0:T(8,128)S(1)}, u32[]{:S(2)}, u32[]{:S(2)}) %collective-permute-start.1) | collective-permute-done | bytes 4128 | tf_op jit(solution)/shard_map/ppermute | solution.py:166
  12.0 0.7 %collective-permute-start.4 = (f32[8,128]{1,0:T(8,128)S(1)}, f32[8,128]{1,0:T(8,128)S(1)}, u32[]{:S(2)}, u32[]{:S(2)}) collective-permute-start(f32[8,128]{1,0:T(8,128)S(1)} %add.70), channel_id=1, source_target_pairs={{0,6},{1,7},{8,14},{9,15},{16,22},{17,23},{24,30},{25,31}} | collective-permute-start | bytes 12296 | tf_op jit(solution)/shard_map/ppermute | solution.py:151
  12.7 1.3 %collective-permute-start.3 = (f32[8,128]{1,0:T(8,128)S(1)}, f32[8,128]{1,0:T(8,128)S(1)}, u32[]{:S(2)}, u32[]{:S(2)}) collective-permute-start(f32[8,128]{1,0:T(8,128)S(1)} %add.70), channel_id=1, source_target_pairs={{0,4},{1,5},{2,6},{3,7},{8,12},{9,13},{10,14},{11,15},{16,20},{17,... | collective-permute-start | bytes 12296 | tf_op jit(solution)/shard_map/ppermute | solution.py:151
  14.0 3.8 %collective-permute-start.2 = (f32[8,128]{1,0:T(8,128)S(1)}, f32[8,128]{1,0:T(8,128)S(1)}, u32[]{:S(2)}, u32[]{:S(2)}) collective-permute-start(f32[8,128]{1,0:T(8,128)S(1)} %add.70), channel_id=1, source_target_pairs={{0,2},{1,3},{2,4},{3,5},{4,6},{5,7},{8,10},{9,11},{10,12},{11,13},... | collective-permute-start | bytes 12296 | tf_op jit(solution)/shard_map/ppermute | solution.py:151
  17.8 0.0 copy-start.2
  17.8 1.4 %convolution_subtract_fusion.w_ref = f32[256,512]{1,0:T(8,128)} fusion(f32[16,256]{1,0:T(8,128)S(1)} %fusion.21, f32[16,512]{1,0:T(8,128)S(1)} %fusion.2, bf16[1,256,512]{2,1,0:T(8,128)(2,1)S(1)} %copy-done.1), kind=kOutput, calls=%fused_computation | convolution fusion | flops 25427968 | bytes 835584 | tf_op jit(solution)/shard_map/dot_general | solution.py:223
  19.2 0.0 collective-permute-done.4
  19.2 0.3 collective-permute-done.3
  19.5 1.0 %collective-permute-done.2 = f32[8,128]{1,0:T(8,128)S(1)} collective-permute-done((f32[8,128]{1,0:T(8,128)S(1)}, f32[8,128]{1,0:T(8,128)S(1)}, u32[]{:S(2)}, u32[]{:S(2)}) %collective-permute-start.2) | collective-permute-done | bytes 4128 | tf_op jit(solution)/shard_map/ppermute | solution.py:151
  20.6 2.3 %collective-permute-start.5 = (f32[2,8,128]{2,1,0:T(8,128)S(1)}, f32[2,8,128]{2,1,0:T(8,128)S(1)}, u32[]{:S(2)}, u32[]{:S(2)}) collective-permute-start(f32[2,8,128]{2,1,0:T(8,128)S(1)} %pad_maximum_fusion), channel_id=1, source_target_pairs={{0,1},{1,0},{2,3},{3,2},{4,5},{5,4},{6,7},{7,6},{8,9},{9,8},{10,11... | collective-permute-start | bytes 24584 | tf_op jit(solution)/shard_map/ppermute | solution.py:139
  22.9 0.0 collective-permute-done.6
  22.9 0.0 copy-done.2
  22.9 0.7 %collective-permute-start.9 = (f32[128,256]{1,0:T(8,128)S(1)}, f32[128,256]{1,0:T(8,128)S(1)}, u32[]{:S(2)}, u32[]{:S(2)}) collective-permute-start(f32[128,256]{1,0:T(8,128)S(1)} %multiply_add_fusion.2), channel_id=1, source_target_pairs={{0,6},{1,7},{8,14},{9,15},{16,22},{17,23},{24,30},{25,31}} | collective-permute-start | bytes 393224 | tf_op jit(solution)/shard_map/ppermute | solution.py:151
  23.6 1.3 %collective-permute-start.8 = (f32[128,256]{1,0:T(8,128)S(1)}, f32[128,256]{1,0:T(8,128)S(1)}, u32[]{:S(2)}, u32[]{:S(2)}) collective-permute-start(f32[128,256]{1,0:T(8,128)S(1)} %multiply_add_fusion.2), channel_id=1, source_target_pairs={{0,4},{1,5},{2,6},{3,7},{8,12},{9,13},{10,14},{11,15},{16,20},{17,... | collective-permute-start | bytes 393224 | tf_op jit(solution)/shard_map/ppermute | solution.py:151
  24.9 2.2 %collective-permute-start.7 = (f32[128,256]{1,0:T(8,128)S(1)}, f32[128,256]{1,0:T(8,128)S(1)}, u32[]{:S(2)}, u32[]{:S(2)}) collective-permute-start(f32[128,256]{1,0:T(8,128)S(1)} %multiply_add_fusion.2), channel_id=1, source_target_pairs={{0,2},{1,3},{2,4},{3,5},{4,6},{5,7},{8,10},{9,11},{10,12},{11,13},... | collective-permute-start | bytes 393224 | tf_op jit(solution)/shard_map/ppermute | solution.py:151
  27.1 0.0 collective-permute-done.5
  27.1 0.0 collective-permute-done.9
  27.1 5.8 %collective-permute-done.8 = f32[128,256]{1,0:T(8,128)S(1)} collective-permute-done((f32[128,256]{1,0:T(8,128)S(1)}, f32[128,256]{1,0:T(8,128)S(1)}, u32[]{:S(2)}, u32[]{:S(2)}) %collective-permute-start.8) | collective-permute-done | bytes 131104 | tf_op jit(solution)/shard_map/ppermute | solution.py:151
  33.0 6.0 %collective-permute-done.7 = f32[128,256]{1,0:T(8,128)S(1)} collective-permute-done((f32[128,256]{1,0:T(8,128)S(1)}, f32[128,256]{1,0:T(8,128)S(1)}, u32[]{:S(2)}, u32[]{:S(2)}) %collective-permute-start.7) | collective-permute-done | bytes 131104 | tf_op jit(solution)/shard_map/ppermute | solution.py:151
  39.0 0.7 %broadcast_select_fusion = (f32[128,256]{1,0:T(8,128)S(1)}, f32[128,256]{1,0:T(8,128)}) fusion(pred[]{:T(512)S(6)} %eq.24, f32[128,256]{1,0:T(8,128)S(1)} %multiply_add_fusion.2, f32[128,256]{1,0:T(8,128)S(1)} %collective-permute-done.6, f32[128,256]{1,0:T(8,128)S(1)} %copy-done.2, f32[128,256]{1,0:T(8,128)S(1)} %collective-permute-done.9, ...), kind=kLoop, calls=%fused_computation.8 | loop fusion | flops 360448 | bytes 1048577 | tf_op jit(solution)/shard_map/jit(_where)/select_n | solution.py:206
  39.7 0.4 collective-permute-start.10
  40.2 0.6 %fusion.13.band_ref = f32[8,128]{1,0:T(8,128)} fusion(f32[2,8,128]{2,1,0:T(8,128)S(1)} %get-tuple-element.14, f32[2,8,128]{2,1,0:T(8,128)S(1)} %get-tuple-element.13, pred[]{:T(512)S(6)} %eq.24), kind=kLoop, calls=%fused_computation.32 | loop fusion | flops 9216 | bytes 20481 | tf_op jit(solution)/shard_map/add | solution.py:216
  40.8 0.4 collective-permute-done.10.other_ref
  41.1 0.7 %copy-done.4 = f32[128,256]{1,0:T(8,128)} copy-done((f32[128,256]{1,0:T(8,128)}, f32[128,256]{1,0:T(8,128)S(1)}, u32[]{:S(2)}) %copy-start.4) | copy-done | bytes 131096
  41.8 4.6 %whiten.1 = f32[256,512]{1,0:T(8,128)} custom-call(s32[1]{0:T(128)} %bitcast.parity_ref, f32[8,128]{1,0:T(8,128)} %fusion.13.band_ref, f32[128,256]{1,0:T(8,128)} %get-tuple-element.12.own_ref, f32[128,256]{1,0:T(8,128)} %copy-done.4, f32[256,512]{1,0:T(8,128)} %convolution_subtract_fusion.w_ref), custom_call_target="tpu_custom_call" | custom-call | flops 1207959552 | bytes 1048576 | tf_op jit(solution)/shard_map/whiten/pallas_call | solution.py:225
  (10 shorter events, 0.1 us)
Async XLA Ops:
  0.0 4.2 %copy-start = (f32[64]{0:T(128)S(1)}, f32[64]{0:T(128)}, u32[]{:S(2)}) copy-start(f32[64]{0:T(128)} %param.5) | copy-start | bytes 772
  0.0 4.2 %copy-start.5 = (s32[1,8]{1,0:T(1,128)S(1)}, s32[1,8]{1,0:T(1,128)}, u32[]{:S(2)}) copy-start(s32[1,8]{1,0:T(1,128)} %param.4) | copy-start | bytes 100
  2.0 7.7 %copy-start.1 = (bf16[1,256,512]{2,1,0:T(8,128)(2,1)S(1)}, bf16[1,256,512]{2,1,0:T(8,128)(2,1)}, u32[]{:S(2)}) copy-start(bf16[1,256,512]{2,1,0:T(8,128)(2,1)} %param.3) | copy-start | bytes 786436
  2.0 7.0 %collective-permute-start = (f32[8,128]{1,0:T(8,128)}, f32[8,128]{1,0:T(8,128)S(1)}, u32[]{:S(2)}, u32[]{:S(2)}) collective-permute-start(f32[8,128]{1,0:T(8,128)} %get-tuple-element.8), channel_id=1, source_target_pairs={{0,8},{8,0},{16,24},{24,16},{1,9},{9,1},{17,25},{25,17},{2,10},{10... | collective-permute-start | bytes 12296 | tf_op jit(solution)/shard_map/ppermute | solution.py:166
  3.3 19.6 %collective-permute-start.6 = (f32[128,256]{1,0:T(8,128)}, f32[128,256]{1,0:T(8,128)S(1)}, u32[]{:S(2)}, u32[]{:S(2)}) collective-permute-start(f32[128,256]{1,0:T(8,128)} %get-tuple-element.10), channel_id=1, source_target_pairs={{0,1},{1,0},{2,3},{3,2},{4,5},{5,4},{6,7},{7,6},{8,9},{9,8},{10,11... | collective-permute-start | bytes 393224 | tf_op jit(solution)/shard_map/ppermute | solution.py:139
  8.8 0.7 %copy-start.3 = (f32[8,128]{1,0:T(8,128)S(1)}, f32[8,128]{1,0:T(8,128)}, u32[]{:S(2)}) copy-start(f32[8,128]{1,0:T(8,128)} %get-tuple-element.8) | copy-start | bytes 12292
  9.5 2.5 %collective-permute-start.1 = (f32[8,128]{1,0:T(8,128)S(1)}, f32[8,128]{1,0:T(8,128)S(1)}, u32[]{:S(2)}, u32[]{:S(2)}) collective-permute-start(f32[8,128]{1,0:T(8,128)S(1)} %add.69), channel_id=1, source_target_pairs={{0,16},{8,24},{16,0},{24,8},{1,17},{9,25},{17,1},{25,9},{2,18},{10... | collective-permute-start | bytes 12296 | tf_op jit(solution)/shard_map/ppermute | solution.py:166
  12.0 7.2 %collective-permute-start.4 = (f32[8,128]{1,0:T(8,128)S(1)}, f32[8,128]{1,0:T(8,128)S(1)}, u32[]{:S(2)}, u32[]{:S(2)}) collective-permute-start(f32[8,128]{1,0:T(8,128)S(1)} %add.70), channel_id=1, source_target_pairs={{0,6},{1,7},{8,14},{9,15},{16,22},{17,23},{24,30},{25,31}} | collective-permute-start | bytes 12296 | tf_op jit(solution)/shard_map/ppermute | solution.py:151
  12.7 6.9 %collective-permute-start.3 = (f32[8,128]{1,0:T(8,128)S(1)}, f32[8,128]{1,0:T(8,128)S(1)}, u32[]{:S(2)}, u32[]{:S(2)}) collective-permute-start(f32[8,128]{1,0:T(8,128)S(1)} %add.70), channel_id=1, source_target_pairs={{0,4},{1,5},{2,6},{3,7},{8,12},{9,13},{10,14},{11,15},{16,20},{17,... | collective-permute-start | bytes 12296 | tf_op jit(solution)/shard_map/ppermute | solution.py:151
  14.0 6.6 %collective-permute-start.2 = (f32[8,128]{1,0:T(8,128)S(1)}, f32[8,128]{1,0:T(8,128)S(1)}, u32[]{:S(2)}, u32[]{:S(2)}) collective-permute-start(f32[8,128]{1,0:T(8,128)S(1)} %add.70), channel_id=1, source_target_pairs={{0,2},{1,3},{2,4},{3,5},{4,6},{5,7},{8,10},{9,11},{10,12},{11,13},... | collective-permute-start | bytes 12296 | tf_op jit(solution)/shard_map/ppermute | solution.py:151
  17.8 5.1 %copy-start.2 = (f32[128,256]{1,0:T(8,128)S(1)}, f32[128,256]{1,0:T(8,128)}, u32[]{:S(2)}) copy-start(f32[128,256]{1,0:T(8,128)} %get-tuple-element.9) | copy-start | bytes 393220
  20.6 6.5 %collective-permute-start.5 = (f32[2,8,128]{2,1,0:T(8,128)S(1)}, f32[2,8,128]{2,1,0:T(8,128)S(1)}, u32[]{:S(2)}, u32[]{:S(2)}) collective-permute-start(f32[2,8,128]{2,1,0:T(8,128)S(1)} %pad_maximum_fusion), channel_id=1, source_target_pairs={{0,1},{1,0},{2,3},{3,2},{4,5},{5,4},{6,7},{7,6},{8,9},{9,8},{10,11... | collective-permute-start | bytes 24584 | tf_op jit(solution)/shard_map/ppermute | solution.py:139
  22.9 4.2 %collective-permute-start.9 = (f32[128,256]{1,0:T(8,128)S(1)}, f32[128,256]{1,0:T(8,128)S(1)}, u32[]{:S(2)}, u32[]{:S(2)}) collective-permute-start(f32[128,256]{1,0:T(8,128)S(1)} %multiply_add_fusion.2), channel_id=1, source_target_pairs={{0,6},{1,7},{8,14},{9,15},{16,22},{17,23},{24,30},{25,31}} | collective-permute-start | bytes 393224 | tf_op jit(solution)/shard_map/ppermute | solution.py:151
  23.6 9.4 %collective-permute-start.8 = (f32[128,256]{1,0:T(8,128)S(1)}, f32[128,256]{1,0:T(8,128)S(1)}, u32[]{:S(2)}, u32[]{:S(2)}) collective-permute-start(f32[128,256]{1,0:T(8,128)S(1)} %multiply_add_fusion.2), channel_id=1, source_target_pairs={{0,4},{1,5},{2,6},{3,7},{8,12},{9,13},{10,14},{11,15},{16,20},{17,... | collective-permute-start | bytes 393224 | tf_op jit(solution)/shard_map/ppermute | solution.py:151
  24.9 14.1 %collective-permute-start.7 = (f32[128,256]{1,0:T(8,128)S(1)}, f32[128,256]{1,0:T(8,128)S(1)}, u32[]{:S(2)}, u32[]{:S(2)}) collective-permute-start(f32[128,256]{1,0:T(8,128)S(1)} %multiply_add_fusion.2), channel_id=1, source_target_pairs={{0,2},{1,3},{2,4},{3,5},{4,6},{5,7},{8,10},{9,11},{10,12},{11,13},... | collective-permute-start | bytes 393224 | tf_op jit(solution)/shard_map/ppermute | solution.py:151
  39.7 1.4 %collective-permute-start.10 = (f32[128,256]{1,0:T(8,128)S(1)}, f32[128,256]{1,0:T(8,128)S(1)}, u32[]{:S(2)}, u32[]{:S(2)}) collective-permute-start(f32[128,256]{1,0:T(8,128)S(1)} %get-tuple-element.11), channel_id=1, source_target_pairs={{0,1},{1,0},{2,3},{3,2},{4,5},{5,4},{6,7},{7,6},{8,9},{9,8},{10,11... | collective-permute-start | bytes 393224 | tf_op jit(solution)/shard_map/ppermute | solution.py:139
  41.1 0.7 %copy-start.4 = (f32[128,256]{1,0:T(8,128)}, f32[128,256]{1,0:T(8,128)S(1)}, u32[]{:S(2)}) copy-start(f32[128,256]{1,0:T(8,128)S(1)} %collective-permute-done.10.other_ref) | copy-start | bytes 393220

commit v2 on v1

--- a/solution.py
+++ b/solution.py
@@ -4,6 +4,7 @@
 from jax.experimental import pallas as pl
 from jax.experimental.pallas import tpu as pltpu
 from jax.sharding import PartitionSpec as P
+
 
 SEG = 256
 HORIZON = 256
@@ -16,6 +17,7 @@
 BF16 = jnp.bfloat16
 VM = pl.BlockSpec(memory_space=pltpu.VMEM)
 SM = pl.BlockSpec(memory_space=pltpu.SMEM)
+PARAMS = pltpu.CompilerParams(vmem_limit_bytes=24 * 2**20)
 
 
 def gram_kernel(parity_ref, volts_ref, keep_ref, give_ref, power_ref, mixed_ref):
@@ -57,19 +59,6 @@
     )
 
 
-def stacked(high_low, first, second):
-    return tuple(
-        jnp.concatenate(
-            [
-                jnp.concatenate([part[first], part[second]], axis=1),
-                jnp.concatenate([part[second], -part[first]], axis=1),
-            ],
-            axis=0,
-        )
-        for part in high_low
-    )
-
-
 def whiten_kernel(parity_ref, band_ref, own_ref, other_ref, w_ref, out_ref, mixed_ref):
     half, antennas = own_ref.shape
     parity = parity_ref[0]
@@ -115,24 +104,65 @@
     out_ref[:, right] = omega * (w_v + 2.0 * v - step[samples:])
 
 
-def steering_rows(angle_sel, antennas):
-    position = jnp.arange(antennas).astype(F32)
-    phase = jnp.pi * jnp.sin(angle_sel)[:, None] * position[None, :]
-    norming = jnp.sqrt(jnp.asarray(antennas, F32))
-    real_part = jnp.cos(phase) / norming
-    imag_part = jnp.sin(phase) / norming
-    upper = jnp.concatenate([real_part, imag_part], axis=1)
-    lower = jnp.concatenate([-imag_part, real_part], axis=1)
-    return jnp.concatenate([upper, lower], axis=0)
-
-
-def null_factor(steer_rows):
-    count = steer_rows.shape[0]
-    steer_gram = jnp.dot(steer_rows, steer_rows.T, precision=PRECISE) + STEER_LOADING * jnp.eye(
-        count, dtype=F32
-    )
-    chol_gram = jnp.linalg.cholesky(steer_gram)
-    return jax.scipy.linalg.solve_triangular(chol_gram, steer_rows, lower=True)
+def complex_inverse(re, im):
+    size = re.shape[0]
+    row = lax.broadcasted_iota(jnp.int32, re.shape, 0)
+    column = lax.broadcasted_iota(jnp.int32, re.shape, 1)
+    for j in range(size):
+        here = column[:1] == j
+        col_re, col_im = re[:, j : j + 1], im[:, j : j + 1]
+        scale = 1.0 / re[j : j + 1, j : j + 1]
+        row_re = jnp.where(here, scale, re[j : j + 1] * scale)
+        row_im = jnp.where(here, 0.0, im[j : j + 1] * scale)
+        rest_re, rest_im = jnp.where(column == j, 0.0, re), jnp.where(column == j, 0.0, im)
+        rest_re = rest_re - (col_re * row_re - col_im * row_im)
+        rest_im = rest_im - (col_re * row_im + col_im * row_re)
+        re = jnp.where(row == j, row_re, rest_re)
+        im = jnp.where(row == j, row_im, rest_im)
+    return re, im
+
+
+def across(left, right):
+    return lax.dot_general(
+        left, right, (((1,), (1,)), ((), ())), precision=PRECISE, preferred_element_type=F32
+    )
+
+
+def null_kernel(picks_ref, angles_ref, volts_ref, out_ref):
+    antennas = volts_ref.shape[1] // 2
+    count = picks_ref.shape[1]
+    row = lax.broadcasted_iota(jnp.int32, (count, 128), 0)
+    angle = jnp.zeros((count, 128), F32)
+    for k in range(count):
+        angle = jnp.where(row == k, angles_ref[picks_ref[0, k]], angle)
+    turn = (jnp.pi * jnp.sin(angle))[:, :1]
+    position = lax.broadcasted_iota(jnp.int32, (count, antennas), 1).astype(F32)
+    phase = turn * position
+    norming = antennas**0.5
+    re, im = jnp.cos(phase) / norming, jnp.sin(phase) / norming
+    both = jnp.concatenate([re, im], axis=1)
+    turned = jnp.concatenate([-im, re], axis=1)
+    eye = lax.broadcasted_iota(jnp.int32, (count, count), 0) == lax.broadcasted_iota(
+        jnp.int32, (count, count), 1
+    )
+    gram_re = across(both, both) + jnp.where(eye, STEER_LOADING, 0.0)
+    gram_im = across(both, turned)
+    inv_re, inv_im = complex_inverse(gram_re, gram_im)
+    steer = jnp.concatenate([both, turned], axis=0)
+    inverse = jnp.concatenate(
+        [
+            jnp.concatenate([inv_re, inv_im], axis=1),
+            jnp.concatenate([-inv_im, inv_re], axis=1),
+        ],
+        axis=0,
+    )
+    back = jnp.dot(inverse, steer, precision=PRECISE, preferred_element_type=F32)
+    volts = volts_ref[...]
+    nt = (((1,), (1,)), ((), ()))
+    inner = sum(
+        lax.dot_general(volts, part, nt, preferred_element_type=F32) for part in split(steer)
+    )
+    out_ref[...] = volts.astype(F32) - dot3(split(inner), split(back))
 
 
 def swap_cores(value, members):
@@ -163,12 +193,13 @@
         return lax.psum(value, "chan")
     step = 1
     while step < groups:
-        value = value + lax.ppermute(value, "chan", [(i, i ^ step) for i in range(groups)])
+        got = lax.ppermute(value, "chan", [(i, i ^ step) for i in range(groups)])
+        value = value + got
         step *= 2
     return value
 
 
-def on_device(volts, picks, angles):
+def steps(volts, picks, angles):
     voltage = volts[0]
     rows, width = voltage.shape
     antennas = width // 2
@@ -193,6 +224,7 @@
         cost_estimate=pl.CostEstimate(
             flops=4 * rows * width * antennas, bytes_accessed=rows * width * 2, transcendentals=0
         ),
+        compiler_params=PARAMS,
         name="segment_gram",
     )(parity, voltage)
 
@@ -215,12 +247,17 @@
     level_own = jnp.where(is_odd, decay * level_own + level_odd[0], level_own)
     band = level_own / lax.axis_size("chan") + TINY_LEVEL
 
-    selector = (picks[0][:, None] == jnp.arange(angles.shape[0], dtype=jnp.int32)[None, :]).astype(F32)
-    angle_sel = jnp.dot(selector, angles, precision=PRECISE)
-    null_rows = null_factor(steering_rows(angle_sel, antennas))
-    volt_float = voltage.astype(F32)
-    inner = jnp.dot(volt_float, null_rows.T, precision=PRECISE)
-    projected = volt_float - jnp.dot(inner, null_rows, precision=PRECISE)
+    projected = pl.pallas_call(
+        null_kernel,
+        out_shape=jax.ShapeDtypeStruct((rows, width), F32),
+        in_specs=[SM, SM, VM],
+        out_specs=VM,
+        cost_estimate=pl.CostEstimate(
+            flops=4 * rows * width * 128, bytes_accessed=rows * width * 6, transcendentals=0
+        ),
+        compiler_params=PARAMS,
+        name="null",
+    )(picks, angles, voltage)
 
     cleaned = pl.pallas_call(
         whiten_kernel,
@@ -231,6 +268,7 @@
         cost_estimate=pl.CostEstimate(
             flops=18 * rows * width * width, bytes_accessed=rows * width * 8, transcendentals=0
         ),
+        compiler_params=PARAMS,
         name="whiten",
     )(parity, band, own, other, projected)
     return cleaned[None]
@@ -239,5 +277,5 @@
 def solution(mesh):
     placed = (P("chan", "tm", None), P("chan", None), P())
     return jax.shard_map(
-        on_device, mesh=mesh, in_specs=placed, out_specs=P("chan", "tm", None), check_vma=False
-    )
+        steps, mesh=mesh, in_specs=placed, out_specs=P("chan", "tm", None), check_vma=False
+    )

time: 46.7 us -> 40.5 us (0.87)
  other arithmetic: 5.49 us -> 0.11 us
  starting transfers between devices: 15.1 us -> 18.2 us
  matrix products: 2.3 us -> 0 us
  waiting for transfers between devices: 15.6 us -> 14.6 us
    another operation x7 -> x2, other arithmetic: 4.02 us -> 0.01 us  [steps(): got_level = swap_cores(jnp.stack([level, level_before]), members)]
    ppermute x3, starting transfers between devices: 3.71 us -> 6.73 us  [swap_cores(): return lax.ppermute(value, 'tm', [(i, i ^ 1) for i in range(members)])]
    dot_general x4 -> x0, matrix products: 2.08 us -> none  [the longest x1 1.42 us: on_device(): projected = volt_float - jnp.dot(inner, null_rows, precision=PRECISE)]
    ppermute x6, waiting for transfers between devices: 13.2 us -> 12.2 us  [earlier_chips(): lax.ppermute(window, 'tm', [(i, i + shift) for i in range(members - shift)])]
    select_n x2, other arithmetic: 0.71 us -> 0.07 us  [the longest x1 0.06 us: steps(): other = swap_cores(jnp.where(is_odd, even_cov, odd_cov), members)]
    ppermute x3, waiting for transfers between devices: 0.39 us -> 0.98 us  [swap_cores(): return lax.ppermute(value, 'tm', [(i, i ^ 1) for i in range(members)])]
    add x4, other arithmetic: 0.62 us -> 0.03 us  [the longest x1 0.02 us: steps(): pair = mine * keep + theirs * got]
    ppermute x2, waiting for transfers between devices: 1.95 us -> 1.37 us  [sum_groups(): got = lax.ppermute(value, 'chan', [(i, i ^ step) for i in range(groups)])]
  transfers between devices with their start and end apart: 11 -> 11, of which waited for: 6 -> 6; matrix products, arithmetic and copies ran while one was open for 15% -> 0% of each run, Pallas kernels for 0% -> 6%
where the time goes in v2:
time: 40.5 us; the launch traced here: 40.2 us
  starting transfers between devices  18.2 us (45%)
  waiting for transfers between devices  14.6 us (36%)
  Pallas kernels  6.25 us (15%)
  local copies, waits for them, and re-layouts  0.96 us (2%)
    ppermute x6, waiting for transfers between devices, earlier_chips(): lax.ppermute(window, 'tm', [(i, i + shift) for i in range(members - shift)])  12.2 us
    ppermute x6, starting transfers between devices, earlier_chips(): lax.ppermute(window, 'tm', [(i, i + shift) for i in range(members - shift)])  9.93 us
    ppermute x3, starting transfers between devices, swap_cores(): return lax.ppermute(value, 'tm', [(i, i ^ 1) for i in range(members)])  6.73 us
    pallas_call x1, Pallas kernels, steps(): pl.pallas_call(whiten_kernel, out_shape=jax.ShapeDtypeStruct((rows, width...  3.44 us
    pallas_call x1, Pallas kernels, steps(): pl.pallas_call(null_kernel, out_shape=jax.ShapeDtypeStruct((rows, width),...  2.36 us
    ppermute x2, starting transfers between devices, sum_groups(): got = lax.ppermute(value, 'chan', [(i, i ^ step) for i in range(groups)])  1.5 us
    ppermute x2, waiting for transfers between devices, sum_groups(): got = lax.ppermute(value, 'chan', [(i, i ^ step) for i in range(groups)])  1.37 us
    ppermute x3, waiting for transfers between devices, swap_cores(): return lax.ppermute(value, 'tm', [(i, i ^ 1) for i in range(members)])  0.98 us
  transfers between devices with their start and end apart: 11, of which 6 were waited for; matrix products, arithmetic and copies ran while one was open for 0% of the time, Pallas kernels for 6%

profile of v2, /device:TPU:21, one launch (start us, length us, event | category | flops | bytes accessed | tf_op | source)
XLA Modules:
  0.0 40.2 jit_solution(9828927339182326444)
XLA Ops:
  0.0 0.0 copy-start
  0.0 0.9 %copy-done = bf16[1,256,512]{2,1,0:T(8,128)(2,1)S(1)} copy-done((bf16[1,256,512]{2,1,0:T(8,128)(2,1)S(1)}, bf16[1,256,512]{2,1,0:T(8,128)(2,1)}, u32[]{:S(2)}) %copy-start) | copy-done | bytes 262168
  1.0 0.0 copy-start.1
  1.0 0.5 %segment_gram.1 = (f32[128,256]{1,0:T(8,128)S(1)}, f32[128,256]{1,0:T(8,128)S(1)}, f32[8,128]{1,0:T(8,128)S(1)}) custom-call(s32[1]{0:T(128)} %bitcast.parity_ref, bf16[256,512]{1,0:T(8,128)(2,1)S(1)} %bitcast.20), custom_call_target="tpu_custom_call" | custom-call | flops 134217728 | bytes 262144 | tf_op jit(solution)/shard_map/segment_gram/pallas_call | solution.py:214
  1.4 1.3 %collective-permute-start = (f32[8,128]{1,0:T(8,128)S(1)}, f32[8,128]{1,0:T(8,128)S(1)}, u32[]{:S(2)}, u32[]{:S(2)}) collective-permute-start(f32[8,128]{1,0:T(8,128)S(1)} %get-tuple-element.8), channel_id=1, source_target_pairs={{0,8},{8,0},{16,24},{24,16},{1,9},{9,1},{17,25},{25,17},{2,10},{10... | collective-permute-start | bytes 12296 | tf_op jit(solution)/shard_map/ppermute | solution.py:196
  2.7 1.2 %collective-permute-done = f32[8,128]{1,0:T(8,128)S(1)} collective-permute-done((f32[8,128]{1,0:T(8,128)S(1)}, f32[8,128]{1,0:T(8,128)S(1)}, u32[]{:S(2)}, u32[]{:S(2)}) %collective-permute-start) | collective-permute-done | bytes 4128 | tf_op jit(solution)/shard_map/ppermute | solution.py:196
  3.9 0.2 collective-permute-start.1
  4.2 2.1 %collective-permute-start.6 = (f32[128,256]{1,0:T(8,128)S(1)}, f32[128,256]{1,0:T(8,128)S(1)}, u32[]{:S(2)}, u32[]{:S(2)}) collective-permute-start(f32[128,256]{1,0:T(8,128)S(1)} %get-tuple-element.10), channel_id=1, source_target_pairs={{0,1},{1,0},{2,3},{3,2},{4,5},{5,4},{6,7},{7,6},{8,9},{9,8},{10,11... | collective-permute-start | bytes 393224 | tf_op jit(solution)/shard_map/ppermute | solution.py:169
  6.3 0.0 copy-start.2
  6.3 0.0 copy-start.3
  6.3 0.1 collective-permute-done.1
  6.4 0.7 %collective-permute-start.4 = (f32[8,128]{1,0:T(8,128)S(1)}, f32[8,128]{1,0:T(8,128)S(1)}, u32[]{:S(2)}, u32[]{:S(2)}) collective-permute-start(f32[8,128]{1,0:T(8,128)S(1)} %add.52), channel_id=1, source_target_pairs={{0,6},{1,7},{8,14},{9,15},{16,22},{17,23},{24,30},{25,31}} | collective-permute-start | bytes 12296 | tf_op jit(solution)/shard_map/ppermute | solution.py:181
  7.1 1.3 %collective-permute-start.3 = (f32[8,128]{1,0:T(8,128)S(1)}, f32[8,128]{1,0:T(8,128)S(1)}, u32[]{:S(2)}, u32[]{:S(2)}) collective-permute-start(f32[8,128]{1,0:T(8,128)S(1)} %add.52), channel_id=1, source_target_pairs={{0,4},{1,5},{2,6},{3,7},{8,12},{9,13},{10,14},{11,15},{16,20},{17,... | collective-permute-start | bytes 12296 | tf_op jit(solution)/shard_map/ppermute | solution.py:181
  8.4 3.8 %collective-permute-start.2 = (f32[8,128]{1,0:T(8,128)S(1)}, f32[8,128]{1,0:T(8,128)S(1)}, u32[]{:S(2)}, u32[]{:S(2)}) collective-permute-start(f32[8,128]{1,0:T(8,128)S(1)} %add.52), channel_id=1, source_target_pairs={{0,2},{1,3},{2,4},{3,5},{4,6},{5,7},{8,10},{9,11},{10,12},{11,13},... | collective-permute-start | bytes 12296 | tf_op jit(solution)/shard_map/ppermute | solution.py:181
  12.2 0.0 copy-done.1
  12.2 0.0 copy-done.2
  12.2 0.0 copy-done.3
  12.2 2.4 %null.1.w_ref = f32[256,512]{1,0:T(8,128)S(1)} custom-call(s32[1,8]{1,0:T(1,128)S(1)} %copy-done.2, f32[64]{0:T(128)S(1)} %copy-done.3, bf16[256,512]{1,0:T(8,128)(2,1)S(1)} %bitcast.21), custom_call_target="tpu_custom_call" | custom-call | flops 67108864 | bytes 786432 | tf_op jit(solution)/shard_map/null/pallas_call | solution.py:250
  14.6 0.0 collective-permute-done.4
  14.6 0.0 collective-permute-done.3
  14.6 0.4 collective-permute-done.2
  15.0 4.1 %collective-permute-start.5 = (f32[2,8,128]{2,1,0:T(8,128)S(1)}, f32[2,8,128]{2,1,0:T(8,128)S(1)}, u32[]{:S(2)}, u32[]{:S(2)}) collective-permute-start(f32[2,8,128]{2,1,0:T(8,128)S(1)} %pad_maximum_fusion), channel_id=1, source_target_pairs={{0,1},{1,0},{2,3},{3,2},{4,5},{5,4},{6,7},{7,6},{8,9},{9,8},{10,11... | collective-permute-start | bytes 24584 | tf_op jit(solution)/shard_map/ppermute | solution.py:169
  19.1 0.0 collective-permute-done.6
  19.1 0.7 %collective-permute-start.9 = (f32[128,256]{1,0:T(8,128)S(1)}, f32[128,256]{1,0:T(8,128)S(1)}, u32[]{:S(2)}, u32[]{:S(2)}) collective-permute-start(f32[128,256]{1,0:T(8,128)S(1)} %multiply_add_fusion.2), channel_id=1, source_target_pairs={{0,6},{1,7},{8,14},{9,15},{16,22},{17,23},{24,30},{25,31}} | collective-permute-start | bytes 393224 | tf_op jit(solution)/shard_map/ppermute | solution.py:181
  19.8 1.3 %collective-permute-start.8 = (f32[128,256]{1,0:T(8,128)S(1)}, f32[128,256]{1,0:T(8,128)S(1)}, u32[]{:S(2)}, u32[]{:S(2)}) collective-permute-start(f32[128,256]{1,0:T(8,128)S(1)} %multiply_add_fusion.2), channel_id=1, source_target_pairs={{0,4},{1,5},{2,6},{3,7},{8,12},{9,13},{10,14},{11,15},{16,20},{17,... | collective-permute-start | bytes 393224 | tf_op jit(solution)/shard_map/ppermute | solution.py:181
  21.1 2.2 %collective-permute-start.7 = (f32[128,256]{1,0:T(8,128)S(1)}, f32[128,256]{1,0:T(8,128)S(1)}, u32[]{:S(2)}, u32[]{:S(2)}) collective-permute-start(f32[128,256]{1,0:T(8,128)S(1)} %multiply_add_fusion.2), channel_id=1, source_target_pairs={{0,2},{1,3},{2,4},{3,5},{4,6},{5,7},{8,10},{9,11},{10,12},{11,13},... | collective-permute-start | bytes 393224 | tf_op jit(solution)/shard_map/ppermute | solution.py:181
  23.3 0.0 collective-permute-done.5
  23.3 0.0 collective-permute-done.9
  23.4 5.9 %collective-permute-done.8 = f32[128,256]{1,0:T(8,128)S(1)} collective-permute-done((f32[128,256]{1,0:T(8,128)S(1)}, f32[128,256]{1,0:T(8,128)S(1)}, u32[]{:S(2)}, u32[]{:S(2)}) %collective-permute-start.8) | collective-permute-done | bytes 131104 | tf_op jit(solution)/shard_map/ppermute | solution.py:181
  29.2 6.0 %collective-permute-done.7 = f32[128,256]{1,0:T(8,128)S(1)} collective-permute-done((f32[128,256]{1,0:T(8,128)S(1)}, f32[128,256]{1,0:T(8,128)S(1)}, u32[]{:S(2)}, u32[]{:S(2)}) %collective-permute-start.7) | collective-permute-done | bytes 131104 | tf_op jit(solution)/shard_map/ppermute | solution.py:181
  35.2 0.1 broadcast_select_fusion
  35.3 0.5 %collective-permute-start.10 = (f32[128,256]{1,0:T(8,128)S(1)}, f32[128,256]{1,0:T(8,128)S(1)}, u32[]{:S(2)}, u32[]{:S(2)}) collective-permute-start(f32[128,256]{1,0:T(8,128)S(1)} %get-tuple-element.11), channel_id=1, source_target_pairs={{0,1},{1,0},{2,3},{3,2},{4,5},{5,4},{6,7},{7,6},{8,9},{9,8},{10,11... | collective-permute-start | bytes 393224 | tf_op jit(solution)/shard_map/ppermute | solution.py:169
  35.8 1.0 %collective-permute-done.10.other_ref = f32[128,256]{1,0:T(8,128)S(1)} collective-permute-done((f32[128,256]{1,0:T(8,128)S(1)}, f32[128,256]{1,0:T(8,128)S(1)}, u32[]{:S(2)}, u32[]{:S(2)}) %collective-permute-start.10) | collective-permute-done | bytes 131104 | tf_op jit(solution)/shard_map/ppermute | solution.py:169
  36.8 3.4 %whiten.1 = f32[256,512]{1,0:T(8,128)} custom-call(s32[1]{0:T(128)} %bitcast.parity_ref, f32[8,128]{1,0:T(8,128)S(1)} %fusion.3.band_ref, f32[128,256]{1,0:T(8,128)S(1)} %get-tuple-element.12.own_ref, f32[128,256]{1,0:T(8,128)S(1)} %collective-permute-done.10.other_ref, f32[256,512]{1,0:T(8,128)S(1)} %null.1.w_ref), custom_call_target="tpu_custom_call" | custom-call | flops 1207959552 | bytes 1048576 | tf_op jit(solution)/shard_map/whiten/pallas_call | solution.py:262
  (7 shorter events, 0.1 us)
Async XLA Ops:
  0.0 0.9 %copy-start = (bf16[1,256,512]{2,1,0:T(8,128)(2,1)S(1)}, bf16[1,256,512]{2,1,0:T(8,128)(2,1)}, u32[]{:S(2)}) copy-start(bf16[1,256,512]{2,1,0:T(8,128)(2,1)} %param.3) | copy-start | bytes 786436
  1.0 11.3 %copy-start.1 = (bf16[1,256,512]{2,1,0:T(8,128)(2,1)S(1)}, bf16[1,256,512]{2,1,0:T(8,128)(2,1)}, u32[]{:S(2)}) copy-start(bf16[1,256,512]{2,1,0:T(8,128)(2,1)} %param.3) | copy-start | bytes 786436
  1.4 2.5 %collective-permute-start = (f32[8,128]{1,0:T(8,128)S(1)}, f32[8,128]{1,0:T(8,128)S(1)}, u32[]{:S(2)}, u32[]{:S(2)}) collective-permute-start(f32[8,128]{1,0:T(8,128)S(1)} %get-tuple-element.8), channel_id=1, source_target_pairs={{0,8},{8,0},{16,24},{24,16},{1,9},{9,1},{17,25},{25,17},{2,10},{10... | collective-permute-start | bytes 12296 | tf_op jit(solution)/shard_map/ppermute | solution.py:196
  3.9 2.5 %collective-permute-start.1 = (f32[8,128]{1,0:T(8,128)S(1)}, f32[8,128]{1,0:T(8,128)S(1)}, u32[]{:S(2)}, u32[]{:S(2)}) collective-permute-start(f32[8,128]{1,0:T(8,128)S(1)} %add.51), channel_id=1, source_target_pairs={{0,16},{8,24},{16,0},{24,8},{1,17},{9,25},{17,1},{25,9},{2,18},{10... | collective-permute-start | bytes 12296 | tf_op jit(solution)/shard_map/ppermute | solution.py:196
  4.2 15.0 %collective-permute-start.6 = (f32[128,256]{1,0:T(8,128)S(1)}, f32[128,256]{1,0:T(8,128)S(1)}, u32[]{:S(2)}, u32[]{:S(2)}) collective-permute-start(f32[128,256]{1,0:T(8,128)S(1)} %get-tuple-element.10), channel_id=1, source_target_pairs={{0,1},{1,0},{2,3},{3,2},{4,5},{5,4},{6,7},{7,6},{8,9},{9,8},{10,11... | collective-permute-start | bytes 393224 | tf_op jit(solution)/shard_map/ppermute | solution.py:169
  6.3 5.9 %copy-start.2 = (s32[1,8]{1,0:T(1,128)S(1)}, s32[1,8]{1,0:T(1,128)}, u32[]{:S(2)}) copy-start(s32[1,8]{1,0:T(1,128)} %picks_ref.1) | copy-start | bytes 100
  6.3 6.0 %copy-start.3 = (f32[64]{0:T(128)S(1)}, f32[64]{0:T(128)}, u32[]{:S(2)}) copy-start(f32[64]{0:T(128)} %angles_ref.1) | copy-start | bytes 772
  6.4 8.2 %collective-permute-start.4 = (f32[8,128]{1,0:T(8,128)S(1)}, f32[8,128]{1,0:T(8,128)S(1)}, u32[]{:S(2)}, u32[]{:S(2)}) collective-permute-start(f32[8,128]{1,0:T(8,128)S(1)} %add.52), channel_id=1, source_target_pairs={{0,6},{1,7},{8,14},{9,15},{16,22},{17,23},{24,30},{25,31}} | collective-permute-start | bytes 12296 | tf_op jit(solution)/shard_map/ppermute | solution.py:181
  7.1 7.6 %collective-permute-start.3 = (f32[8,128]{1,0:T(8,128)S(1)}, f32[8,128]{1,0:T(8,128)S(1)}, u32[]{:S(2)}, u32[]{:S(2)}) collective-permute-start(f32[8,128]{1,0:T(8,128)S(1)} %add.52), channel_id=1, source_target_pairs={{0,4},{1,5},{2,6},{3,7},{8,12},{9,13},{10,14},{11,15},{16,20},{17,... | collective-permute-start | bytes 12296 | tf_op jit(solution)/shard_map/ppermute | solution.py:181
  8.4 6.6 %collective-permute-start.2 = (f32[8,128]{1,0:T(8,128)S(1)}, f32[8,128]{1,0:T(8,128)S(1)}, u32[]{:S(2)}, u32[]{:S(2)}) collective-permute-start(f32[8,128]{1,0:T(8,128)S(1)} %add.52), channel_id=1, source_target_pairs={{0,2},{1,3},{2,4},{3,5},{4,6},{5,7},{8,10},{9,11},{10,12},{11,13},... | collective-permute-start | bytes 12296 | tf_op jit(solution)/shard_map/ppermute | solution.py:181
  15.0 8.3 %collective-permute-start.5 = (f32[2,8,128]{2,1,0:T(8,128)S(1)}, f32[2,8,128]{2,1,0:T(8,128)S(1)}, u32[]{:S(2)}, u32[]{:S(2)}) collective-permute-start(f32[2,8,128]{2,1,0:T(8,128)S(1)} %pad_maximum_fusion), channel_id=1, source_target_pairs={{0,1},{1,0},{2,3},{3,2},{4,5},{5,4},{6,7},{7,6},{8,9},{9,8},{10,11... | collective-permute-start | bytes 24584 | tf_op jit(solution)/shard_map/ppermute | solution.py:169
  19.1 4.2 %collective-permute-start.9 = (f32[128,256]{1,0:T(8,128)S(1)}, f32[128,256]{1,0:T(8,128)S(1)}, u32[]{:S(2)}, u32[]{:S(2)}) collective-permute-start(f32[128,256]{1,0:T(8,128)S(1)} %multiply_add_fusion.2), channel_id=1, source_target_pairs={{0,6},{1,7},{8,14},{9,15},{16,22},{17,23},{24,30},{25,31}} | collective-permute-start | bytes 393224 | tf_op jit(solution)/shard_map/ppermute | solution.py:181
  19.8 9.4 %collective-permute-start.8 = (f32[128,256]{1,0:T(8,128)S(1)}, f32[128,256]{1,0:T(8,128)S(1)}, u32[]{:S(2)}, u32[]{:S(2)}) collective-permute-start(f32[128,256]{1,0:T(8,128)S(1)} %multiply_add_fusion.2), channel_id=1, source_target_pairs={{0,4},{1,5},{2,6},{3,7},{8,12},{9,13},{10,14},{11,15},{16,20},{17,... | collective-permute-start | bytes 393224 | tf_op jit(solution)/shard_map/ppermute | solution.py:181
  21.1 14.1 %collective-permute-start.7 = (f32[128,256]{1,0:T(8,128)S(1)}, f32[128,256]{1,0:T(8,128)S(1)}, u32[]{:S(2)}, u32[]{:S(2)}) collective-permute-start(f32[128,256]{1,0:T(8,128)S(1)} %multiply_add_fusion.2), channel_id=1, source_target_pairs={{0,2},{1,3},{2,4},{3,5},{4,6},{5,7},{8,10},{9,11},{10,12},{11,13},... | collective-permute-start | bytes 393224 | tf_op jit(solution)/shard_map/ppermute | solution.py:181
  35.3 1.5 %collective-permute-start.10 = (f32[128,256]{1,0:T(8,128)S(1)}, f32[128,256]{1,0:T(8,128)S(1)}, u32[]{:S(2)}, u32[]{:S(2)}) collective-permute-start(f32[128,256]{1,0:T(8,128)S(1)} %get-tuple-element.11), channel_id=1, source_target_pairs={{0,1},{1,0},{2,3},{3,2},{4,5},{5,4},{6,7},{7,6},{8,9},{9,8},{10,11... | collective-permute-start | bytes 393224 | tf_op jit(solution)/shard_map/ppermute | solution.py:169
